TPU v7x, 32 devices: a whole 2x2x4 slice. The times are simulated.
32 devices in a mesh: row: 4 (over y, core), col: 8 (over z, x).
Axes of the slice: x: 2, y: 2, z: 4, core: 2. Of those that a mesh axis runs over, the one named last changes fastest.
Arguments:
- fluid_data: float32 [51, 8192], P(None, ('row', 'col')), as said below
- center_data: float32 [51, 8192], P(None, ('col', 'row')), as said below
- poly_coef: float32 [48, 4], replicated, may hold values from -3 to 3
Outputs:
- fluid_motion: float32 [48, 8192], P(None, ('row', 'col'))
- center_load: float32 [48, 8192], P(None, ('col', 'row'))
Inputs may be any that keep to these rules, and one draw needn't show every extreme that they name: Rows 0 to 2 of fluid_data lie in [0, 1]; rows 3 and on are forces. Rows 0 and 1 of center_data lie in [0, 1] and row 2 lies in [-0.5, -0.02], so every center is at least 0.02 below every vertex; rows 3 and on are coefficients.
All inputs are finite; a program needn't handle non-finite values.
Results may differ from a plain program's by a relative error of at most 0.0003.
Values sent between devices are 32-bit elements; how exact they have to be, the bound alone decides.
A program may use at most 64 MiB of HBM per device.

v0:
```python
import math

import jax
import jax.numpy as jnp
from jax import lax
from jax.sharding import PartitionSpec as P

WAVES = 64


def kernel_block(center_pos, fluid_pos):
    dx = center_pos[0][:, None] - fluid_pos[0][None, :]
    dy = center_pos[1][:, None] - fluid_pos[1][None, :]
    dz = center_pos[2][:, None] - fluid_pos[2][None, :]
    sq = dx * dx + dy * dy + dz * dz
    phase = 2.0 * math.pi * WAVES * jnp.sqrt(sq)
    return jnp.sin(phase) / phase


def both_maps(centers, fluid):
    total = centers.shape[1]
    width = fluid.shape[1]
    block = math.gcd(total, max(128, 2**20 // width))
    count = total // block
    fluid_pos = fluid[:3]
    forces = fluid[3:]
    pieces = centers.reshape(centers.shape[0], count, block).transpose(1, 0, 2)

    def step(motion, piece):
        tile = kernel_block(piece[:3], fluid_pos)
        motion = motion + jnp.dot(
            piece[3:], tile, precision=lax.Precision.HIGHEST, preferred_element_type=jnp.float32
        )
        back = lax.dot_general(
            forces,
            tile,
            (((1,), (1,)), ((), ())),
            precision=lax.Precision.HIGHEST,
            preferred_element_type=jnp.float32,
        )
        return (motion, back)

    start = jnp.zeros((forces.shape[0], width), jnp.float32)
    motion, backs = lax.scan(step, start, pieces)
    loads = backs.transpose(1, 0, 2).reshape(forces.shape[0], total)
    return (motion, loads)


def per_device(fluid_data, center_data, poly_coef):
    fluid_block = lax.all_gather(fluid_data, "col", axis=1, tiled=True)
    center_block = lax.all_gather(center_data, "row", axis=1, tiled=True)
    partial_motion, partial_loads = both_maps(center_block, fluid_block)
    motion = lax.psum_scatter(partial_motion, "col", scatter_dimension=1, tiled=True)
    loads = lax.psum_scatter(partial_loads, "row", scatter_dimension=1, tiled=True)
    affine = poly_coef[:, 0:1] + jnp.dot(
        poly_coef[:, 1:],
        fluid_data[:3],
        precision=lax.Precision.HIGHEST,
        preferred_element_type=jnp.float32,
    )
    return (motion + affine, loads)


def solution(mesh):
    placed = (P(None, ("row", "col")), P(None, ("col", "row")), P())
    return jax.shard_map(
        per_device,
        mesh=mesh,
        in_specs=placed,
        out_specs=(P(None, ("row", "col")), P(None, ("col", "row"))),
        check_vma=False,
    )
```

profile of v0, /device:TPU:0, one launch (start us, length us, event | category | flops | bytes accessed | tf_op | source)
XLA Modules:
  0.0 231.2 jit_solution(7686842501280449595)
XLA Ops:
  7.2 0.0 reduce-scatter.3.cloned.1.call-start
  7.2 33.1 %all_gather.7 = f32[51,2048]{1,0:T(8,128)S(1)} all-gather(f32[51,256]{1,0:T(8,128)} %param.5), channel_id=1, replica_groups=mesh['row'=4,'col'=8] {'col'}, dimensions={1}, use_global_device_ids=true | all-gather | bytes 470016 | tf_op jit(solution)/shard_map/all_gather | solution.py:50
  40.3 0.0 copy-start.1
  40.4 0.7 copy-done.1
  41.1 5.7 %all_gather.6 = f32[51,1024]{1,0:T(8,128)S(1)} all-gather(f32[51,256]{1,0:T(8,128)S(1)} %copy-done.1), channel_id=1, replica_groups=mesh['row'=4,'col'=8] {'row'}, dimensions={1}, use_global_device_ids=true | all-gather | bytes 261120 | tf_op jit(solution)/shard_map/all_gather | solution.py:51
  46.8 0.2 reshape.21
  47.0 89.9 %while.13 = (s32[]{:T(128)}, f32[48,2048]{1,0:T(8,128)S(1)}, f32[2,48,512]{2,1,0:T(8,128)S(1)}, f32[2,51,512]{2,0,1:T(2,128)S(1)}, f32[3,2048]{1,0:T(4,128)S(1)}...) while((s32[]{:T(128)}, f32[48,2048]{1,0:T(8,128)S(1)}, ...), condition=%wide.region_1.2_spmd.clone, body=%wide.region_0.1_spmd.clone.sunk | while | flops 1229127680 | bytes 1695923 | solution.py:44
  47.2 0.1 constant_dynamic-slice_fusion.7
  47.4 19.3 %convolution_add_fusion.3 = f32[48,2048]{1,0:T(8,128)S(1)} fusion(f32[2048]{0:T(1024)S(1)} %bitcast.50, f32[512]{0:T(512)S(1)} %bitcast.59, f32[2048]{0:T(1024)S(1)} %bitcast.52, f32[512]{0:T(512)S(1)} %bitcast.57, f32[2048]{0:T(1024)S(1)} %bitcast.48, f32[512]{0:T(512)S(1)} %bitcast.55, f32[48,2048]{1,0:T(8,128)S(1)} %get-tuple-element.143, ...), kind=kOutput, calls=%fused_computation.1.clone.1 | convolution fusion | flops 614662144 | bytes 915457 | tf_op jit(solution)/shard_map/while/body/eval_jaxpr/dot_general | solution.py:31
  66.7 20.2 %fusion.15 = f32[2,48,512]{2,1,0:T(8,128)S(1)} fusion(f32[2,48,512]{2,1,0:T(8,128)S(1)} %get-tuple-element.144, s32[]{:T(128)} %get-tuple-element.142, f32[48,2048]{1,0:T(8,128)S(1)} %get-tuple-element.158, f32[2048]{0:T(1024)S(1)} %bitcast.51, f32[512]{0:T(512)S(1)} %bitcast.60, f32[2048]{0:T(1024)S(1)} %bitcast.53, f32[512]{0:T(512)S(1)} %bitcast.58, ...), kind=kOutput, calls=%fused_computation.4.clone.1 | convolution fusion | flops 614465536 | bytes 522244 | tf_op jit(solution)/shard_map/while/body/eval_jaxpr/dot_general | solution.py:34
  91.7 0.1 constant_dynamic-slice_fusion.7
  91.9 19.0 %convolution_add_fusion.3 = f32[48,2048]{1,0:T(8,128)S(1)} fusion(f32[2048]{0:T(1024)S(1)} %bitcast.50, f32[512]{0:T(512)S(1)} %bitcast.59, f32[2048]{0:T(1024)S(1)} %bitcast.52, f32[512]{0:T(512)S(1)} %bitcast.57, f32[2048]{0:T(1024)S(1)} %bitcast.48, f32[512]{0:T(512)S(1)} %bitcast.55, f32[48,2048]{1,0:T(8,128)S(1)} %get-tuple-element.143, ...), kind=kOutput, calls=%fused_computation.1.clone.1 | convolution fusion | flops 614662144 | bytes 915457 | tf_op jit(solution)/shard_map/while/body/eval_jaxpr/dot_general | solution.py:31
  110.9 20.5 %fusion.15 = f32[2,48,512]{2,1,0:T(8,128)S(1)} fusion(f32[2,48,512]{2,1,0:T(8,128)S(1)} %get-tuple-element.144, s32[]{:T(128)} %get-tuple-element.142, f32[48,2048]{1,0:T(8,128)S(1)} %get-tuple-element.158, f32[2048]{0:T(1024)S(1)} %bitcast.51, f32[512]{0:T(512)S(1)} %bitcast.60, f32[2048]{0:T(1024)S(1)} %bitcast.53, f32[512]{0:T(512)S(1)} %bitcast.58, ...), kind=kOutput, calls=%fused_computation.4.clone.1 | convolution fusion | flops 614465536 | bytes 522244 | tf_op jit(solution)/shard_map/while/body/eval_jaxpr/dot_general | solution.py:34
  136.9 0.0 copy-start
  136.9 0.0 copy-start.2
  136.9 0.7 copy-done
  137.6 0.0 reduce-scatter.3.cloned.1.call-update
  137.6 0.0 reduce-scatter.5.cloned.1.call-start
  137.7 0.7 copy.13
  138.4 0.0 reduce-scatter.5.cloned.1.call-update
  138.4 0.0 copy-done.2
  138.4 63.8 %reduce-scatter.3.cloned.1.call-done = f32[48,256]{1,0:T(8,128)} async-done(((f32[48,2048]{1,0:T(8,128)}), f32[48,256]{1,0:T(8,128)}) %reduce-scatter.3.cloned.1.call-update) | async-done | bytes 49168 | tf_op jit(solution)/shard_map/reduce_scatter | solution.py:53
  202.3 1.7 fusion.5
  204.0 20.2 %reduce-scatter.5.cloned.1.call-done = f32[48,256]{1,0:T(8,128)} async-done(((f32[48,1024]{1,0:T(8,128)}), f32[48,256]{1,0:T(8,128)}) %reduce-scatter.5.cloned.1.call-update) | async-done | bytes 49168 | tf_op jit(solution)/shard_map/reduce_scatter | solution.py:54
  (9 shorter events, 0.1 us)
Async XLA Ops:
  7.2 195.1 %reduce-scatter.3.cloned.1.call-start = ((), (), s32[]{:S(2)}) async-start(), calls=%async_computation.2 | async-start | bytes 442368 | tf_op jit(solution)/shard_map/reduce_scatter | solution.py:53
  40.3 0.8 copy-start.1
  136.9 0.8 copy-start
  136.9 1.5 copy-start.2
  137.6 86.5 %reduce-scatter.5.cloned.1.call-start = ((), (), s32[]{:S(2)}) async-start(), calls=%async_computation.3 | async-start | bytes 245760 | tf_op jit(solution)/shard_map/reduce_scatter | solution.py:54
Sparse Core Ops, SparseCore 0:
  137.8 64.4 reduce-scatter.2
  205.3 18.7 reduce-scatter.4
where the time goes:
time: 233 us; the launch traced here: 231 us
  waiting for transfers between devices  84 us (36%)
  matrix products  80.7 us (35%)
  blocking collectives  38.8 us (17%)
  between operations  14.3 us (6%)
  loops' own time  10.6 us (5%)
  local copies, waits for them, and re-layouts  2.66 us (1%)
    reduce_scatter x1, waiting for transfers between devices, per_device(): lax.psum_scatter(partial_motion, 'col', scatter_dimension=1, tiled=True)  63.8 us
    dot_general x2, matrix products, step(): lax.dot_general(forces, tile, (((1,), (1,)), ((), ())), precision=lax.Pre...  40.7 us
    dot_general x2, matrix products, step(): jnp.dot(piece[3:], tile, precision=lax.Precision.HIGHEST, preferred_eleme...  38.3 us
    all_gather x1, blocking collectives, per_device(): fluid_block = lax.all_gather(fluid_data, 'col', axis=1, tiled=True)  33.1 us
    reduce_scatter x1, waiting for transfers between devices, per_device(): lax.psum_scatter(partial_loads, 'row', scatter_dimension=1, tiled=True)  20.2 us
    another operation x1, loops' own time, both_maps(): motion, backs = lax.scan(step, start, pieces)  10.6 us
    all_gather x1, blocking collectives, per_device(): center_block = lax.all_gather(center_data, 'row', axis=1, tiled=True)  5.67 us
  transfers between devices with their start and end apart: 2, of which 2 were waited for; matrix products, arithmetic and copies ran while one was open for 1% of the time, Pallas kernels for 0%

commit v1 on v0

v1 whole, which is shorter than its diff:
```python
import functools

import jax
import jax.numpy as jnp
from jax import lax
from jax.experimental import pallas as pl
from jax.experimental.pallas import tpu as pltpu
from jax.sharding import PartitionSpec as P

WAVES = 64
MESH = pl.DeviceIdType.MESH
TOP = 12.404427306735432
MID = 0.6418441597071612
LOW = 0.16126480593510223


def paired(me, m, n):
    if n & (n - 1) == 0:
        other, bit = 0, 1
        while bit < n:
            other = other + (((me // bit) % 2 + (m // bit) % 2) % 2) * bit
            bit *= 2
        return other, other
    return (me + m) % n, (me - m + n) % n


def dot(a, b, dims):
    return lax.dot_general(a, b, (dims, ((), ())), preferred_element_type=jnp.float32)


def split(x):
    high = x.astype(jnp.bfloat16)
    low = (x - high.astype(jnp.float32)).astype(jnp.bfloat16)
    return high, low


def body(rows, cols, side, fluid, center, poly, motion, loads, *scratch):
    fl, ce, cp, chl, fhl, kh, kl, mo_out, mo_in, ld_out, ld_in = scratch[:11]
    fs, fr, cs, cr, ms, mr, ls, lr = scratch[11:]
    S, T = cols // side, rows * side
    row, col = lax.axis_index("row"), lax.axis_index("col")
    my_s, my_t = col // side, (col % side) * rows + row
    nvals = poly.shape[0]
    wf, wc = fluid.shape[1], center.shape[1]
    lanes = 128 if wf % 128 == 0 else wf
    step_rows = 32 if wc % 32 == 0 else wc

    def along_s(m):
        to, src = paired(my_s, m, S)
        return tuple({"row": row, "col": i * side + col % side} for i in (to, src))

    def along_t(m):
        to, src = paired(my_t, m, T)
        return tuple({"row": i % rows, "col": (col // side) * side + i // rows} for i in (to, src))

    def copy(src, dst, send, recv, where):
        return pltpu.make_async_remote_copy(
            src_ref=src, dst_ref=dst, send_sem=send, recv_sem=recv, device_id=where, device_id_type=MESH
        )

    def send_fluid(m):
        return copy(fluid, fl.at[m], fs.at[m], fr.at[m], along_s(m)[0])

    def send_center(m):
        return copy(center, ce.at[m], cs.at[m], cr.at[m], along_t(m)[0])

    def send_motion(m):
        return copy(mo_out.at[m], mo_in.at[m], ms.at[m], mr.at[m], along_s(m)[1])

    def send_loads(m):
        return copy(ld_out.at[m], ld_in.at[m], ls.at[m], lr.at[m], along_t(m)[1])

    barrier = pltpu.get_barrier_semaphore()
    for m in range(1, max(S, T)):
        if m < T:
            pl.semaphore_signal(barrier, inc=1, device_id=along_t(m)[0], device_id_type=MESH)
        if m < S:
            pl.semaphore_signal(barrier, inc=1, device_id=along_s(m)[0], device_id_type=MESH)
    fl[0] = fluid[...]
    ce[0] = center[...]
    pl.semaphore_wait(barrier, S + T - 2)
    for m in range(1, max(S, T)):
        if m < T:
            send_center(m).start()
        if m < S:
            send_fluid(m).start()

    def ready_center(r):
        @pl.when(r > 0)
        def _():
            send_center(r).wait_recv()

        places = jnp.transpose(ce[r, 0:8, :] * float(WAVES))
        for a in range(3):
            cp[r, a] = jnp.broadcast_to(places[:, a : a + 1], (wc, lanes))
        high, low = split(ce[r, 3:, :] * TOP)
        chl[r, 0:nvals] = high
        chl[r, nvals:] = low
        ld_out[r] = jnp.zeros((nvals, wc), jnp.float32)

    def tile(m, r, slot):
        for h in range(wf // lanes):
            part = pl.ds(h * lanes, lanes)
            fx, fy, fz = (fl[m, a : a + 1, part] * float(WAVES) for a in range(3))
            for j in range(0, wc, step_rows):
                at = pl.ds(j, step_rows)
                dx, dy, dz = cp[r, 0, at, :] - fx, cp[r, 1, at, :] - fy, cp[r, 2, at, :] - fz
                sq = dx * dx + dy * dy + dz * dz
                inv = lax.rsqrt(sq)
                turns = sq * inv
                f = turns - jnp.round(turns)
                size = jnp.abs(f)
                rest = 0.5 - size
                q = size * rest
                value = (f * rest * inv) * ((q + MID) * q + LOW)
                high, low = split(value)
                kh[slot, at, part] = high
                kl[slot, at, part] = low
        k_high, k_low = kh[slot], kl[slot]
        across = ((1,), (0,))
        wide = dot(chl[r], k_high, across)
        mo_out[m] += wide[:nvals] + wide[nvals:] + dot(chl[r, 0:nvals], k_low, across)
        back = ((1,), (1,))
        wide = dot(fhl[...], k_high, back)
        ld_out[r] += wide[:nvals] + wide[nvals:] + dot(fhl[0:nvals], k_low, back)

    group = 2 if T % 2 == 0 else 1

    def step(s, _):
        m = (s + 1) % S
        last = s // (S - 1) if S > 1 else 1

        @pl.when(m > 0)
        def _():
            send_fluid(m).wait_recv()

        high, low = split(fl[m, 3:, :] * TOP)
        fhl[0:nvals] = high
        fhl[nvals:] = low
        mo_out[m] = jnp.zeros((nvals, wf), jnp.float32)

        def pair(k, _):
            which = [(k * group + e + last) % T for e in range(group)]

            @pl.when(s == 0)
            def _():
                for r in which:
                    ready_center(r)

            for e, r in enumerate(which):
                tile(m, r, e)

            @pl.when((s > 0) & (k == 0))
            def _():
                send_motion(s).start()

            for r in which:
                @pl.when((s == S - 1) & (r > 0))
                def _():
                    send_loads(r).start()

            return 0

        lax.fori_loop(0, T // group, pair, 0)
        return 0

    lax.fori_loop(0, S, step, 0)

    total = mo_out[0]
    for a in range(3):
        total = total + poly[:, a + 1 : a + 2] * fluid[a : a + 1, :]
    total = total + poly[:, 0:1]
    for m in range(1, S):
        send_motion(m).wait_recv()
        total = total + mo_in[m]
    motion[...] = total
    total = ld_out[0]
    for m in range(1, T):
        send_loads(m).wait_recv()
        total = total + ld_in[m]
    loads[...] = total
    for m in range(1, S):
        send_fluid(m).wait_send()
        send_motion(m).wait_send()
    for m in range(1, T):
        send_center(m).wait_send()
        send_loads(m).wait_send()


def per_device(rows, cols, side, fluid_data, center_data, poly_coef):
    f32, bf16 = jnp.float32, jnp.bfloat16
    S, T = cols // side, rows * side
    height, wf = fluid_data.shape
    wc = center_data.shape[1]
    n = height - 3
    lanes = 128 if wf % 128 == 0 else wf
    vmem = pl.BlockSpec(memory_space=pltpu.VMEM)
    sems = [pltpu.SemaphoreType.DMA((k,)) for k in (S, S, T, T, S, S, T, T)]
    return pl.pallas_call(
        functools.partial(body, rows, cols, side),
        out_shape=(jax.ShapeDtypeStruct((n, wf), f32), jax.ShapeDtypeStruct((n, wc), f32)),
        in_specs=[vmem] * 3,
        out_specs=(vmem, vmem),
        scratch_shapes=[
            pltpu.VMEM((S, height, wf), f32),
            pltpu.VMEM((T, height, wc), f32),
            pltpu.VMEM((T, 3, wc, lanes), f32),
            pltpu.VMEM((T, 2 * n, wc), bf16),
            pltpu.VMEM((2 * n, wf), bf16),
            pltpu.VMEM((2, wc, wf), bf16),
            pltpu.VMEM((2, wc, wf), bf16),
            pltpu.VMEM((S, n, wf), f32),
            pltpu.VMEM((S, n, wf), f32),
            pltpu.VMEM((T, n, wc), f32),
            pltpu.VMEM((T, n, wc), f32),
            *sems,
        ],
        compiler_params=pltpu.CompilerParams(
            collective_id=0, has_side_effects=True, vmem_limit_bytes=48 * 2**20
        ),
    )(fluid_data, center_data, poly_coef)


def solution(mesh):
    rows, cols = mesh.shape["row"], mesh.shape["col"]
    side = 2 if cols % 2 == 0 else 1
    placed = (P(None, ("row", "col")), P(None, ("col", "row")), P())
    return jax.shard_map(
        functools.partial(per_device, rows, cols, side),
        mesh=mesh,
        in_specs=placed,
        out_specs=(P(None, ("row", "col")), P(None, ("col", "row"))),
        check_vma=False,
    )
```

time: 233 us -> 33.7 us (0.14)
  waiting for transfers between devices: 84 us -> 0 us
  matrix products: 80.7 us -> 0 us
  blocking collectives: 38.8 us -> 0 us
  Pallas kernels: 0 us -> 29.2 us
  between operations: 14.3 us -> 0.64 us
  loops' own time: 10.6 us -> 0 us
    reduce_scatter x2 -> x0, waiting for transfers between devices: 84 us -> none  [the longest x1 63.8 us: per_device(): lax.psum_scatter(partial_motion, 'col', scatter_dimension=1, tiled=True)]
    dot_general x5 -> x0, matrix products: 80.7 us -> none  [the longest x2 40.7 us: step(): lax.dot_general(forces, tile, (((1,), (1,)), ((), ())), precision=lax.Pre...]
    all_gather x2 -> x0, blocking collectives: 38.8 us -> none  [the longest x1 33.1 us: per_device(): fluid_block = lax.all_gather(fluid_data, 'col', axis=1, tiled=True)]
    pallas_call x0 -> x1, Pallas kernels: none -> 29.2 us  [per_device(): pl.pallas_call(functools.partial(body, rows, cols, side), out_shape=(jax....]
    another operation x1 -> x0, loops' own time: 10.6 us -> none  [both_maps(): motion, backs = lax.scan(step, start, pieces)]
  transfers between devices with their start and end apart: 2 -> 0, of which waited for: 2 -> 0; matrix products, arithmetic and copies ran while one was open for 1% -> 0% of each run, Pallas kernels for 0% -> 0%
where the time goes in v1:
time: 33.7 us; the launch traced here: 33.5 us
  Pallas kernels  29.2 us (87%)
  local copies, waits for them, and re-layouts  3.65 us (11%)
  between operations  0.64 us (2%)
    pallas_call x1, Pallas kernels, per_device(): pl.pallas_call(functools.partial(body, rows, cols, side), out_shape=(jax....  29.2 us
    unnamed x7, local copies, waits for them, and re-layouts  3.65 us

profile of v1, /device:TPU:0, one launch (start us, length us, event | category | flops | bytes accessed | tf_op | source)
XLA Modules:
  0.0 33.5 jit_solution(1681974007559644577)
XLA Ops:
  0.6 0.8 %copy.5.poly = f32[48,4]{1,0:T(8,128)S(1)} copy(f32[48,4]{0,1:T(4,128)} %param.5) | data formatting | bytes 1536 | tf_op args[2]
  1.4 0.0 copy-start
  1.4 0.8 %copy-done = f32[51,256]{1,0:T(8,128)S(1)} copy-done((f32[51,256]{1,0:T(8,128)S(1)}, f32[51,256]{1,0:T(8,128)}, u32[]{:S(2)}) %copy-start) | copy-done | bytes 52248
  2.2 0.0 copy-start.1
  2.2 0.8 %copy-done.1 = f32[51,256]{1,0:T(8,128)S(1)} copy-done((f32[51,256]{1,0:T(8,128)S(1)}, f32[51,256]{1,0:T(8,128)}, u32[]{:S(2)}) %copy-start.1) | copy-done | bytes 52248
  3.0 29.2 %shard_map.50 = (f32[48,256]{1,0:T(8,128)S(1)}, f32[48,256]{1,0:T(8,128)S(1)}) custom-call(f32[51,256]{1,0:T(8,128)S(1)} %copy-done, f32[51,256]{1,0:T(8,128)S(1)} %copy-done.1, f32[48,4]{1,0:T(8,128)S(1)} %copy.5.poly), custom_call_target="tpu_custom_call" | custom-call | tf_op jit(solution)/shard_map/pallas_call | solution.py:199
  32.2 0.6 %copy.8 = f32[48,256]{1,0:T(8,128)} copy(f32[48,256]{1,0:T(8,128)S(1)} %get-tuple-element.4) | data formatting | bytes 98304
  32.8 0.6 %copy.9 = f32[48,256]{1,0:T(8,128)} copy(f32[48,256]{1,0:T(8,128)S(1)} %get-tuple-element.5) | data formatting | bytes 98304
Async XLA Ops:
  1.4 0.8 %copy-start = (f32[51,256]{1,0:T(8,128)S(1)}, f32[51,256]{1,0:T(8,128)}, u32[]{:S(2)}) copy-start(f32[51,256]{1,0:T(8,128)} %fluid.1) | copy-start | bytes 156676
  2.2 0.8 %copy-start.1 = (f32[51,256]{1,0:T(8,128)S(1)}, f32[51,256]{1,0:T(8,128)}, u32[]{:S(2)}) copy-start(f32[51,256]{1,0:T(8,128)} %center.1) | copy-start | bytes 156676

commit v2 on v1

v2 whole, which is shorter than its diff:
```python
import functools

import jax
import jax.numpy as jnp
from jax import lax
from jax.experimental import pallas as pl
from jax.experimental.pallas import tpu as pltpu
from jax.sharding import PartitionSpec as P

WAVES = 64
MESH = pl.DeviceIdType.MESH
TOP = 12.404427306735432
MID = 0.6418441597071612
LOW = 0.16126480593510223


def paired(me, m, n):
    other, bit = 0, 1
    while bit < n:
        other = other + (((me // bit) % 2 + (m // bit) % 2) % 2) * bit
        bit *= 2
    return other


def dot(a, b, dims):
    return lax.dot_general(a, b, (dims, ((), ())), preferred_element_type=jnp.float32)


def split(x):
    high = x.astype(jnp.bfloat16)
    low = (x - high.astype(jnp.float32)).astype(jnp.bfloat16)
    return high, low


def body(rows, cols, side, fluid, center, poly, motion, loads, *scratch):
    fl, ce, pv, cp, chl, fhl, kh, kl, mo_out, mo_in, ld_out, ld_in, pre = scratch[:13]
    own, fs, fr, cs, cr, ms, mr, ls, lr, ps, pr = scratch[13:]
    S, T = cols // side, rows * side
    half = T // 2
    row, col = lax.axis_index("row"), lax.axis_index("col")
    my_s, my_t = col // side, (row % 2) * half + (col % side) * (rows // 2) + row // 2
    nvals = pv.shape[1]
    wf, wc = fluid.shape[1], center.shape[1]
    lanes = 128 if wf % 128 == 0 else wf
    step_rows = 32 if wc % 32 == 0 else wc

    def along_s(m):
        return {"row": row, "col": paired(my_s, m, S) * side + col % side}

    def along_t(m):
        i = paired(my_t, m, T)
        return {
            "row": (i % (rows // 2)) * 2 + i // half,
            "col": (col // side) * side + (i % half) // (rows // 2),
        }

    def copy(src, dst, send, recv, where):
        return pltpu.make_async_remote_copy(
            src_ref=src, dst_ref=dst, send_sem=send, recv_sem=recv, device_id=where, device_id_type=MESH
        )

    def send_fluid(m):
        return copy(fl.at[0], fl.at[m], fs.at[m], fr.at[m], along_s(m))

    def send_center(p):
        return copy(ce.at[0], ce.at[p], cs.at[p], cr.at[p], along_t(half if p == 1 else p - 1))

    def hand_on(p):
        q = p + half - 1
        return copy(ce.at[p], ce.at[q], cs.at[q], cr.at[q], along_t(half))

    def send_motion(m):
        return copy(mo_out.at[m], mo_in.at[m], ms.at[m], mr.at[m], along_s(m))

    def send_pre(p):
        j = p - half
        return copy(ld_out.at[p], pre.at[j], ps.at[j], pr.at[j], along_t(half))

    def send_loads(j):
        return copy(ld_out.at[j + 1], ld_in.at[j], ls.at[j], lr.at[j], along_t(j))

    def send_other():
        return copy(ld_out.at[1], ld_in.at[0], ls.at[0], lr.at[0], along_t(half))

    local = [
        pltpu.make_async_copy(center, ce.at[0], own.at[0]),
        pltpu.make_async_copy(fluid, fl.at[0], own.at[1]),
        pltpu.make_async_copy(poly, pv, own.at[2]),
    ]
    for c in local:
        c.start()
    barrier = pltpu.get_barrier_semaphore()
    for p in range(1, half + 1):
        pl.semaphore_signal(barrier, inc=1, device_id=along_t(p), device_id_type=MESH)
    for m in range(1, S):
        pl.semaphore_signal(barrier, inc=1, device_id=along_s(m), device_id_type=MESH)
    for c in local:
        c.wait()
    order_s = [1] + list(range(S - 1, 1, -1))
    pl.semaphore_wait(barrier, S - 1 + half)
    for p in range(1, half + 1):
        send_center(p).start()
    for m in order_s:
        send_fluid(m).start()

    def ready_center(r):
        places = jnp.transpose(ce[r, 0:8, :] * float(WAVES))
        for a in range(3):
            cp[r, a] = jnp.broadcast_to(places[:, a : a + 1], (wc, lanes))
        high, low = split(ce[r, 3:, :] * TOP)
        chl[r, 0:nvals] = high
        chl[r, nvals:] = low
        ld_out[r] = jnp.zeros((nvals, wc), jnp.float32)

    def ready_fluid(m):
        high, low = split(fl[m, 3:, :] * TOP)
        fhl[m, 0:nvals] = high
        fhl[m, nvals:] = low
        mo_out[m] = jnp.zeros((nvals, wf), jnp.float32)

    def values(m, r, slot):
        for h in range(wf // lanes):
            part = pl.ds(h * lanes, lanes)
            fx, fy, fz = (fl[m, a : a + 1, part] * float(WAVES) for a in range(3))
            for j in range(0, wc, step_rows):
                at = pl.ds(j, step_rows)
                dx, dy, dz = cp[r, 0, at, :] - fx, cp[r, 1, at, :] - fy, cp[r, 2, at, :] - fz
                sq = dx * dx + dy * dy + dz * dz
                inv = lax.rsqrt(sq)
                turns = sq * inv
                f = turns - jnp.round(turns)
                size = jnp.abs(f)
                rest = 0.5 - size
                q = size * rest
                value = (f * rest * inv) * ((q + MID) * q + LOW)
                high, low = split(value)
                kh[slot, at, part] = high
                kl[slot, at, part] = low

    def sums(m, r, slot):
        k_high, k_low = kh[slot], kl[slot]
        across = ((1,), (0,))
        wide = dot(chl[r], k_high, across)
        mo_out[m] += wide[:nvals] + wide[nvals:] + dot(chl[r, 0:nvals], k_low, across)
        back = ((1,), (1,))
        wide = dot(fhl[m], k_high, back)
        ld_out[r] += wide[:nvals] + wide[nvals:] + dot(fhl[m, 0:nvals], k_low, back)

    def pair(before, one, two):
        sums(*before, 1)
        values(*one, 0)
        sums(*one, 0)
        values(*two, 1)
        return two

    kh[1] = jnp.zeros((wc, wf), jnp.bfloat16)
    kl[1] = jnp.zeros((wc, wf), jnp.bfloat16)
    ready_fluid(0)
    before = (0, 0)

    for k in range(half):
        for p in (2 * k, 2 * k + 1):
            if 2 <= p <= half:
                send_center(p).wait_recv()
                hand_on(p).start()
            elif p == 1:
                send_center(p).wait_recv()
            elif p > half:
                hand_on(p - half + 1).wait_recv()
            ready_center(p)
        if k == 0:
            send_fluid(order_s[0]).wait_recv()
            ready_fluid(order_s[0])
        m = order_s[0]
        before = pair(before, (m, 2 * k), (m, 2 * k + 1))

    def middle(s, _):
        m = S - s
        send_fluid(m).wait_recv()
        ready_fluid(m)
        last_m = (m + 1) % S + (m + 1) // S

        pair((last_m, T - 1), (m, 0), (m, 1))
        send_motion(last_m).start()

        def inner(k, _):
            pair((m, 2 * k - 1), (m, 2 * k), (m, 2 * k + 1))
            return 0

        lax.fori_loop(1, half, inner, 0)
        return 0

    lax.fori_loop(1, S - 2, middle, 0)

    far = order_s[-1]
    prior = order_s[-2]
    send_fluid(far).wait_recv()
    ready_fluid(far)
    pair((prior, T - 1), (far, T - 1), (0, T - 1))
    send_motion(prior).start()

    def mixed(k, _):
        r = T - 1 - k
        pair((0, r + 1), (far, r), (0, r))
        send_pre(r + 1).start()
        return 0

    lax.fori_loop(1, half, mixed, 0)

    def finish(j):
        send_pre(half + j).wait_recv()
        ld_out[j + 1] += pre[j]
        send_loads(j).start()

    pair((0, half), (far, half - 1), (far, half - 2))
    finish(half - 1)

    def far_rest(k, _):
        r = half - 1 - 2 * k
        pair((far, r + 1), (far, r), (far, r - 1))
        return 0

    lax.fori_loop(1, half // 2, far_rest, 0)
    pair((far, 0), (0, half - 1), (0, half - 2))
    send_motion(far).start()
    finish(half - 2)

    def own_rest(k, _):
        r = half - 1 - 2 * k
        pair((0, r + 1), (0, r), (0, r - 1))
        finish(r)

        @pl.when(r > 1)
        def _():
            finish(r - 1)

        return 0

    lax.fori_loop(1, half // 2, own_rest, 0)
    send_other().start()
    sums(0, 0, 1)

    total = mo_out[0]
    affine = jnp.transpose(pv[...])
    for a in range(3):
        total = total + affine[:, a + 1 : a + 2] * fl[0, a : a + 1, :]
    total = total + affine[:, 0:1]
    for m in order_s:
        send_motion(m).wait_recv()
        total = total + mo_in[m]
    motion[...] = total
    total = ld_out[0]
    for j in range(half - 1, 0, -1):
        send_loads(j).wait_recv()
        total = total + ld_in[j]
    send_other().wait_recv()
    loads[...] = total + ld_in[0]
    for m in order_s:
        send_fluid(m).wait_send()
        send_motion(m).wait_send()
    for p in range(1, half + 1):
        send_center(p).wait_send()
    for p in range(2, half + 1):
        hand_on(p).wait_send()
        send_pre(p + half - 1).wait_send()
        send_loads(p - 1).wait_send()
    send_other().wait_send()


def per_device(rows, cols, side, fluid_data, center_data, poly_coef):
    f32, bf16 = jnp.float32, jnp.bfloat16
    S, T = cols // side, rows * side
    height, wf = fluid_data.shape
    wc = center_data.shape[1]
    n = height - 3
    lanes = 128 if wf % 128 == 0 else wf
    vmem = pl.BlockSpec(memory_space=pltpu.VMEM)
    hbm = pl.BlockSpec(memory_space=pltpu.HBM)
    sems = [pltpu.SemaphoreType.DMA((k,)) for k in (3, S, S, T, T, S, S, T // 2, T // 2, T // 2, T // 2)]
    return pl.pallas_call(
        functools.partial(body, rows, cols, side),
        out_shape=(jax.ShapeDtypeStruct((n, wf), f32), jax.ShapeDtypeStruct((n, wc), f32)),
        in_specs=[hbm] * 3,
        out_specs=(vmem, vmem),
        scratch_shapes=[
            pltpu.VMEM((S, height, wf), f32),
            pltpu.VMEM((T, height, wc), f32),
            pltpu.VMEM((4, n), f32),
            pltpu.VMEM((T, 3, wc, lanes), f32),
            pltpu.VMEM((T, 2 * n, wc), bf16),
            pltpu.VMEM((S, 2 * n, wf), bf16),
            pltpu.VMEM((2, wc, wf), bf16),
            pltpu.VMEM((2, wc, wf), bf16),
            pltpu.VMEM((S, n, wf), f32),
            pltpu.VMEM((S, n, wf), f32),
            pltpu.VMEM((T, n, wc), f32),
            pltpu.VMEM((T // 2, n, wc), f32),
            pltpu.VMEM((T // 2, n, wc), f32),
            *sems,
        ],
        compiler_params=pltpu.CompilerParams(
            collective_id=0, has_side_effects=True, vmem_limit_bytes=48 * 2**20
        ),
    )(fluid_data, center_data, poly_coef.T)


def solution(mesh):
    rows, cols = mesh.shape["row"], mesh.shape["col"]
    side = 2 if cols % 2 == 0 else 1
    placed = (P(None, ("row", "col")), P(None, ("col", "row")), P())
    return jax.shard_map(
        functools.partial(per_device, rows, cols, side),
        mesh=mesh,
        in_specs=placed,
        out_specs=(P(None, ("row", "col")), P(None, ("col", "row"))),
        check_vma=False,
    )
```

time: 33.7 us -> 30.1 us (0.89)
  Pallas kernels: 29.2 us -> 25.6 us
    pallas_call x1, Pallas kernels: 29.2 us -> 25.6 us  [per_device(): pl.pallas_call(functools.partial(body, rows, cols, side), out_shape=(jax....]
    unnamed x7 -> x8, local copies, waits for them, and re-layouts: 3.65 us -> 3.55 us
where the time goes in v2:
time: 30.1 us; the launch traced here: 29.8 us
  Pallas kernels  25.6 us (85%)
  local copies, waits for them, and re-layouts  3.55 us (12%)
  between operations  0.65 us (2%)
    pallas_call x1, Pallas kernels, per_device(): pl.pallas_call(functools.partial(body, rows, cols, side), out_shape=(jax....  25.6 us
    unnamed x8, local copies, waits for them, and re-layouts  3.55 us

profile of v2, /device:TPU:0, one launch (start us, length us, event | category | flops | bytes accessed | tf_op | source)
XLA Modules:
  0.0 29.8 jit_solution(4436089609950344113)
XLA Ops:
  0.6 0.0 copy-start
  0.6 0.8 %copy-done = f32[51,256]{1,0:T(8,128)S(1)} copy-done((f32[51,256]{1,0:T(8,128)S(1)}, f32[51,256]{1,0:T(8,128)}, u32[]{:S(2)}) %copy-start) | copy-done | bytes 52248
  1.4 0.0 copy-start.1
  1.5 0.8 %copy-done.1 = f32[51,256]{1,0:T(8,128)S(1)} copy-done((f32[51,256]{1,0:T(8,128)S(1)}, f32[51,256]{1,0:T(8,128)}, u32[]{:S(2)}) %copy-start.1) | copy-done | bytes 52248
  2.3 0.0 copy-start.2
  2.3 0.7 %copy-done.2 = f32[48,4]{0,1:T(4,128)S(1)} copy-done((f32[48,4]{0,1:T(4,128)S(1)}, f32[48,4]{0,1:T(4,128)}, u32[]{:S(2)}) %copy-start.2) | copy-done | bytes 792
  3.0 25.6 %shard_map.50 = (f32[48,256]{1,0:T(8,128)S(1)}, f32[48,256]{1,0:T(8,128)S(1)}) custom-call(f32[51,256]{1,0:T(8,128)S(1)} %copy-done, f32[51,256]{1,0:T(8,128)S(1)} %copy-done.1, f32[4,48]{1,0:T(4,128)S(1)} %bitcast.1), custom_call_target="tpu_custom_call" | custom-call | tf_op jit(solution)/shard_map/pallas_call | solution.py:280
  28.6 0.6 %copy.7 = f32[48,256]{1,0:T(8,128)} copy(f32[48,256]{1,0:T(8,128)S(1)} %get-tuple-element.4) | data formatting | bytes 98304
  29.2 0.6 %copy.8 = f32[48,256]{1,0:T(8,128)} copy(f32[48,256]{1,0:T(8,128)S(1)} %get-tuple-element.5) | data formatting | bytes 98304
Async XLA Ops:
  0.6 0.8 %copy-start = (f32[51,256]{1,0:T(8,128)S(1)}, f32[51,256]{1,0:T(8,128)}, u32[]{:S(2)}) copy-start(f32[51,256]{1,0:T(8,128)} %fluid.1) | copy-start | bytes 156676
  1.4 0.8 %copy-start.1 = (f32[51,256]{1,0:T(8,128)S(1)}, f32[51,256]{1,0:T(8,128)}, u32[]{:S(2)}) copy-start(f32[51,256]{1,0:T(8,128)} %center.1) | copy-start | bytes 156676
  2.3 0.7 %copy-start.2 = (f32[48,4]{0,1:T(4,128)S(1)}, f32[48,4]{0,1:T(4,128)}, u32[]{:S(2)}) copy-start(f32[48,4]{0,1:T(4,128)} %param.5) | copy-start | bytes 2308
